TPU v7x, 512 devices: a whole 4x8x8 slice. The times are simulated.
512 devices in a mesh: facet: 16 (over x_hi, z), col: 32 (over y, x_lo, core).
Axes of the slice: x: 4 (x_hi: 2, x_lo: 2; x = x_hi * 2 + x_lo), y: 8, z: 8, core: 2. Of those that a mesh axis runs over, the one named last changes fastest.
Arguments:
- facets: bfloat16 [16, 256, 2, 128], P('facet', 'col'), may hold values from -6 to 6
- sub_offsets: int32 [32, 16], P('col'), may hold values from 0 to 8191
- col_offsets: int32 [32], P('col'), may hold values from 0 to 8191
- screen_index: int32 [32, 16], P('col', 'facet'), may hold values from 0 to 3
- screens: float32 [4, 2, 256, 256], replicated, may hold values from -6 to 6
Outputs:
- facets_out: float32 [16, 256, 2, 128], P('facet', 'col')
All inputs are finite; a program needn't handle non-finite values.
Results may differ from a plain program's by a relative error of at most 0.0056.
Values may be sent and summed in bfloat16 or wider, within the bound.
A program may use at most 64 MiB of HBM per device.

v0:
```python
import functools
import math

import jax
import jax.numpy as jnp
import numpy as np
from jax import lax
from jax.experimental import pallas as pl
from jax.experimental.pallas import tpu as pltpu
from jax.sharding import PartitionSpec as P

XC = 64
XS = 256
SLAB = 128
NPAD = 8192
STEP = 7
ROWS = 8
SPAN = 176
MESH = pl.DeviceIdType.MESH
F32 = jnp.float32
BF16 = jnp.bfloat16


def fourier_tables(facets):
    a = np.arange(XS)[:, None]
    q = np.arange(XS)[None, :]
    angle = 2.0 * np.pi * ((a * q) % XS) / XS
    keep = (q < STEP * (facets - 1) + XC).astype(np.float64)
    re = np.cos(angle) / math.sqrt(XS) * keep
    im = np.sin(angle) / math.sqrt(XS) * keep
    row_in = np.block([[re.T, im.T], [-im.T, re.T]])
    col_in = np.concatenate([re, im], axis=0) / math.sqrt(facets)
    col_out = np.concatenate([re.T[:SPAN], im.T[:SPAN]], axis=0)
    row_out = np.block([[re, -im], [im, re]])
    return tuple(jnp.asarray(t, dtype=BF16) for t in (row_in, col_in, col_out, row_out))


def unit_circle(n):
    n = n & (NPAD - 1)
    quarter = (n + NPAD // 8) >> 11
    t = (n - (quarter << 11)).astype(F32) * (2.0 * math.pi / NPAD)
    t2 = t * t
    c = 1.0 + t2 * (-1.0 / 2 + t2 * (1.0 / 24 + t2 * (-1.0 / 720 + t2 * (1.0 / 40320))))
    s = t * (1.0 + t2 * (-1.0 / 6 + t2 * (1.0 / 120 + t2 * (-1.0 / 5040 + t2 * (1.0 / 362880)))))
    odd = (quarter & 1) == 1
    cos = jnp.where(odd, s, c)
    sin = jnp.where(odd, c, s)
    cos = jnp.where(((quarter + 1) & 2) == 2, -cos, cos)
    sin = jnp.where((quarter & 2) == 2, -sin, sin)
    return cos, sin


def iota(shape, dim):
    return lax.broadcasted_iota(jnp.int32, shape, dim)


def join_parts(t):
    rows = t.shape[0]
    even = (iota(t.shape, 0) & 1) == 0
    low = iota(t.shape, 1) < XC
    other = jnp.where(even, pltpu.roll(t, rows - 1, 0), pltpu.roll(t, 1, 0))
    other = pltpu.roll(other, XC, 1)
    return jnp.where(even == low, t - other, t + other)


def dot(a, b):
    return jnp.dot(a, b, preferred_element_type=F32)


def kernel(
    nf,
    nc,
    x_hbm,
    sub_hbm,
    col_hbm,
    idx_hbm,
    screens_hbm,
    row_in_hbm,
    col_in_hbm,
    col_out_hbm,
    row_out_hbm,
    out_ref,
    sub_s,
    col_s,
    idx_s,
    screens,
    row_in,
    col_in,
    col_out,
    row_out,
    slab,
    phase,
    phase_t,
    across,
    across_t,
    c_out,
    c_in,
    z,
    half,
    w,
    r_out,
    r_in,
    t_out,
    t_in,
    local_sem,
    slab_send,
    slab_recv,
    c_send,
    c_recv,
    r_send,
    r_recv,
    t_send,
    t_recv,
):
    me_f = lax.axis_index("facet")
    me_c = lax.axis_index("col")
    height = ROWS * nc
    block = 2 * ROWS

    def slab_rows(j):
        return pl.ds(pl.multiple_of(j * block, block), block)

    def sub_rows(s):
        return pl.ds(pl.multiple_of(s * XC, XC), XC)

    local = [
        pltpu.make_async_copy(src, dst, local_sem.at[i])
        for i, (src, dst) in enumerate(
            [
                (x_hbm, slab.at[slab_rows(me_c)]),
                (sub_hbm, sub_s),
                (col_hbm, col_s),
                (idx_hbm, idx_s),
                (screens_hbm, screens),
                (row_in_hbm, row_in),
                (col_in_hbm, col_in),
                (col_out_hbm, col_out),
                (row_out_hbm, row_out),
            ]
        )
    ]
    for copy in local:
        copy.start()

    barrier = pltpu.get_barrier_semaphore()

    def greet(axis, me, peers):
        def one(k, carry):
            pl.semaphore_signal(
                barrier, 1, device_id={axis: lax.rem(me + k, peers)}, device_id_type=MESH
            )
            return carry

        lax.fori_loop(1, peers, one, 0)

    greet("col", me_c, nc)
    greet("facet", me_f, nf)

    for copy in local[1:4]:
        copy.wait()
    offset = col_s[0, 0]
    lane = iota((SLAB, 2 * XC), 1)
    cos, sin = unit_circle(iota((SLAB, 2 * XC), 0) * (offset + (lane & (XC - 1))))
    across[...] = (jnp.where(lane < XC, cos, -sin) * (1.0 / math.sqrt(SLAB))).astype(BF16)
    part = iota((2 * XC, SLAB), 0)
    cos, sin = unit_circle(iota((2 * XC, SLAB), 1) * (offset + (part & (XC - 1))))
    across_t[...] = (jnp.where(part < XC, cos, -sin) * (1.0 / math.sqrt(SLAB))).astype(BF16)

    local[0].wait()
    pl.semaphore_wait(barrier, nc - 1 + nf - 1)

    def remote(src, dst, send, recv, axis, peer):
        return pltpu.make_async_remote_copy(
            src_ref=src,
            dst_ref=dst,
            send_sem=send,
            recv_sem=recv,
            device_id={axis: peer},
            device_id_type=MESH,
        )

    def send_slab(k, carry):
        mine = slab.at[slab_rows(me_c)]
        remote(mine, mine, slab_send, slab_recv, "col", lax.rem(me_c + k, nc)).start()
        return carry

    lax.fori_loop(1, nc, send_slab, 0)

    lane_row = (8, 2 * height)
    place = iota(lane_row, 1)
    row_id = me_f * height + (place >> 1)
    turn = (place & 1) * (NPAD // 4)
    within = iota((XC, 2 * height), 0)
    place_u = iota((XC, 2 * height), 1)
    cos_u, sin_u = unit_circle(within * (me_f * height + (place_u >> 1)))
    cos_u = cos_u.reshape(XC // 8, 8, 2 * height)
    sin_u = sin_u.reshape(XC // 8, 8, 2 * height)

    def fill_phase(s, carry):
        cos_s, sin_s = unit_circle(sub_s[0, s] * row_id - turn)
        scale = 1.0 / math.sqrt(height)
        values = (cos_s * scale)[None] * cos_u - (sin_s * scale)[None] * sin_u
        phase[sub_rows(s), :] = values.reshape(XC, 2 * height).astype(BF16)
        return carry

    lax.fori_loop(0, nf, fill_phase, 0)

    tall = (2 * height, 2 * XC)
    row_t = me_f * height + (iota(tall, 0) >> 1)
    turn_t = (iota(tall, 0) & 1) * (NPAD // 4)
    lane_t = iota(tall, 1)

    def fill_phase_t(t, carry):
        freq = jnp.where(lane_t < XC, sub_s[0, 2 * t], sub_s[0, 2 * t + 1]) + (lane_t & (XC - 1))
        cos_t, _ = unit_circle(freq * row_t - turn_t)
        columns = pl.ds(pl.multiple_of(t * 2 * XC, 2 * XC), 2 * XC)
        phase_t[:, columns] = (cos_t * (1.0 / math.sqrt(height))).astype(BF16)
        return carry

    lax.fori_loop(0, nf // 2, fill_phase_t, 0)
    z[...] = jnp.zeros_like(z)
    half[...] = jnp.zeros_like(half)
    for copy in local[4:]:
        copy.wait()

    others = slab.at[pl.ds(0, (nc - 1) * block)]
    arrival = remote(others, others, slab_send, slab_recv, "col", me_c)
    arrival.wait_send()
    arrival.wait_recv()

    spread = join_parts(dot(slab[...], across[...])).astype(BF16)
    c_out[...] = dot(phase[...], spread).astype(BF16)

    def send_c(k, carry):
        peer = lax.rem(me_f + k, nf)
        remote(
            c_out.at[sub_rows(peer)], c_in.at[sub_rows(me_f)], c_send, c_recv.at[me_f], "facet", peer
        ).start()
        return carry

    lax.fori_loop(1, nf, send_c, 0)
    c_in[sub_rows(me_f), :] = c_out[sub_rows(me_f), :]

    lane_c = iota((XC, 2 * XC), 1)
    for f in range(nf):
        start = STEP * f
        rows = pl.ds(start, XC)

        @pl.when(f != me_f)
        def _():
            slot = c_in.at[pl.ds(f * XC, XC)]
            remote(slot, slot, c_send, c_recv.at[f], "facet", me_f).wait_recv()

        got = c_in[pl.ds(f * XC, XC), :].astype(F32)
        re = pltpu.roll(got, start, 1) if start else got
        im = pltpu.roll(got, (start + XC) % (2 * XC), 1)
        first = (lane_c >= start) & (lane_c < start + XC)
        z[rows, 0:128] += jnp.where(first, re, 0.0)
        z[rows, 256:384] += jnp.where(first, im, 0.0)
        if start + XC > 128:
            second = lane_c < start + XC - 128
            z[rows, 128:256] += jnp.where(second, re, 0.0)
            z[rows, 384:512] += jnp.where(second, im, 0.0)

    half[0:SPAN, :] = dot(z[...].astype(BF16), row_in[...]).astype(BF16)
    grid = dot(col_in[...], half[...])
    sub_re = grid[0:XS, 0:XS] - grid[XS:, XS:]
    sub_im = grid[0:XS, XS:] + grid[XS:, 0:XS]
    g = idx_s[0, 0]
    gain_re = screens[g, 0]
    gain_im = screens[g, 1]
    screened = jnp.concatenate(
        [
            (sub_re * gain_re - sub_im * gain_im).astype(BF16),
            (sub_re * gain_im + sub_im * gain_re).astype(BF16),
        ],
        axis=1,
    )
    inner = dot(col_out[...], screened)
    inner = jnp.concatenate(
        [
            (inner[0:SPAN, 0:XS] + inner[SPAN:, XS:]).astype(BF16),
            (inner[0:SPAN, XS:] - inner[SPAN:, 0:XS]).astype(BF16),
        ],
        axis=1,
    )
    w[...] = dot(inner, row_out[...])

    for f in range(nf):
        start = STEP * f
        rows = pl.ds(start, XC)
        re = w[rows, 0:128]
        im = w[rows, 256:384]
        if start + XC > 128:
            re = jnp.where(lane_c >= start, re, w[rows, 128:256])
            im = jnp.where(lane_c >= start, im, w[rows, 384:512])
        re = pltpu.roll(re, 128 - start, 1) if start else re
        im = pltpu.roll(im, (XC + 128 - start) % 128, 1)
        r_out[pl.ds(f * XC, XC), :] = jnp.where(lane_c < XC, re, im).astype(BF16)

    def send_r(k, carry):
        peer = lax.rem(me_f + k, nf)
        remote(
            r_out.at[sub_rows(peer)], r_in.at[sub_rows(me_f)], r_send, r_recv, "facet", peer
        ).start()
        return carry

    lax.fori_loop(1, nf, send_r, 0)
    r_in[sub_rows(me_f), :] = r_out[sub_rows(me_f), :]

    others = r_in.at[pl.ds(0, (nf - 1) * XC)]
    remote(others, others, r_send, r_recv, "facet", me_f).wait_recv()

    rows = join_parts(dot(phase_t[...], r_in[...])).astype(BF16)
    t_out[...] = dot(rows, across_t[...]).astype(BF16)

    def send_t(k, carry):
        peer = lax.rem(me_c + k, nc)
        remote(
            t_out.at[slab_rows(peer)], t_in.at[slab_rows(me_c)], t_send, t_recv, "col", peer
        ).start()
        return carry

    lax.fori_loop(1, nc, send_t, 0)
    t_in[slab_rows(me_c), :] = t_out[slab_rows(me_c), :]

    others = c_in.at[pl.ds(0, (nf - 1) * XC)]
    remote(others, others, c_send, r_recv, "facet", me_f).wait_send()
    remote(others, others, r_send, r_recv, "facet", me_f).wait_send()
    others = t_in.at[pl.ds(0, (nc - 1) * block)]
    arrival = remote(others, others, t_send, t_recv, "col", me_c)
    arrival.wait_send()
    arrival.wait_recv()

    total = jnp.sum(t_in[...].astype(F32).reshape(nc, block, SLAB), axis=0)
    out_ref[...] = total * (1.0 / math.sqrt(nc * nf))


def body(nf, nc, facets, sub_offsets, col_offsets, screen_index, screens):
    block = 2 * ROWS
    height = ROWS * nc
    tables = fourier_tables(nf)
    hbm = pl.BlockSpec(memory_space=pltpu.HBM)
    vmem = pltpu.VMEM
    dma = pltpu.SemaphoreType.DMA
    out = pl.pallas_call(
        functools.partial(kernel, nf, nc),
        name="swiftly",
        out_shape=jax.ShapeDtypeStruct((block, SLAB), F32),
        in_specs=[hbm] * 9,
        out_specs=pl.BlockSpec(memory_space=pltpu.VMEM),
        scratch_shapes=[
            pltpu.SMEM((1, nf), jnp.int32),
            pltpu.SMEM((1, 1), jnp.int32),
            pltpu.SMEM((1, 1), jnp.int32),
            vmem(screens.shape, F32),
            *[vmem(t.shape, BF16) for t in tables],
            vmem((2 * height, SLAB), BF16),
            vmem((nf * XC, 2 * height), BF16),
            vmem((2 * height, nf * XC), BF16),
            vmem((SLAB, 2 * XC), BF16),
            vmem((2 * XC, SLAB), BF16),
            vmem((nf * XC, 2 * XC), BF16),
            vmem((nf * XC, 2 * XC), BF16),
            vmem((SPAN, 2 * XS), F32),
            vmem((XS, 2 * XS), BF16),
            vmem((SPAN, 2 * XS), F32),
            vmem((nf * XC, 2 * XC), BF16),
            vmem((nf * XC, 2 * XC), BF16),
            vmem((2 * height, SLAB), BF16),
            vmem((2 * height, SLAB), BF16),
            dma((9,)),
            dma,
            dma,
            dma,
            dma((nf,)),
            dma,
            dma,
            dma,
            dma,
        ],
        compiler_params=pltpu.CompilerParams(collective_id=0, has_side_effects=True),
    )(
        facets.reshape(block, SLAB),
        sub_offsets,
        col_offsets.reshape(1, 1),
        screen_index,
        screens,
        *tables,
    )
    return out.reshape(1, ROWS, 2, SLAB)


def solution(mesh):
    return jax.shard_map(
        functools.partial(body, mesh.shape["facet"], mesh.shape["col"]),
        mesh=mesh,
        in_specs=(P("facet", "col", None, None), P("col", None), P("col"), P("col", "facet"), P()),
        out_specs=P("facet", "col", None, None),
        check_vma=False,
    )
```

profile of v0, /device:TPU:1, one launch (start us, length us, event | category | flops | bytes accessed | tf_op | source)
XLA Modules:
  0.0 54.1 jit_solution(15030285561075994453)
XLA Ops:
  1.3 51.4 %swiftly.1 = f32[16,128]{1,0:T(8,128)} custom-call(bf16[16,128]{1,0:T(8,128)(2,1)} %bitcast.5, s32[1,16]{1,0:T(1,128)} %sub_hbm.1, s32[1,1]{1,0:T(1,128)} %bitcast.3.col_hbm, s32[1,1]{1,0:T(1,128)S(6)} %copy.12.idx_hbm, f32[4,2,256,256]{3,2,1,0:T(8,128)} %screens_hbm.1, bf16[512,512]{1,0:T(8,128)(2,1)} %constant.8.clone.row_in_hbm, ...), custom_call_target="tpu_custom_call" | custom-call | tf_op jit(solution)/shard_map/swiftly/pallas_call | solution.py:346
  52.8 1.3 %copy.13 = f32[1,8,2,128]{3,2,1,0:T(2,128)} copy(f32[1,8,2,128]{3,2,1,0:T(2,128)} %bitcast.4) | data formatting | bytes 16384
where the time goes:
time: 54.2 us; the launch traced here: 54.1 us
  Pallas kernels  51.4 us (95%)
  local copies, waits for them, and re-layouts  1.3 us (2%)
  between operations  1.3 us (2%)
    pallas_call x1, Pallas kernels, body(): pl.pallas_call(functools.partial(kernel, nf, nc), name='swiftly', out_sha...  51.4 us
    unnamed x1, local copies, waits for them, and re-layouts  1.3 us

commit v1 on v0

--- a/solution.py
+++ b/solution.py
@@ -65,6 +65,22 @@
 
 def dot(a, b):
     return jnp.dot(a, b, preferred_element_type=F32)
+
+
+def peers_of_col(me, count):
+    ny = count // 4
+    steps = [(dy, low) for dy in range(ny) for low in range(4) if dy or low]
+    steps.sort(key=lambda k: -(min(k[0], ny - k[0]) + (k[1] >> 1)))
+    y, rest = me >> 2, me & 3
+    return [lax.rem(y + dy, ny) * 4 + (rest ^ low) for dy, low in steps]
+
+
+def peers_of_facet(me, count):
+    nz = count // 2
+    steps = [(dx, dz) for dx in range(2) for dz in range(nz) if dx or dz]
+    steps.sort(key=lambda k: -(min(k[1], nz - k[1]) + 2 * k[0]))
+    x, z = me // nz, lax.rem(me, nz)
+    return [(x ^ dx) * nz + lax.rem(z + dz, nz) for dx, dz in steps]
 
 
 def kernel(
@@ -114,6 +130,8 @@
 ):
     me_f = lax.axis_index("facet")
     me_c = lax.axis_index("col")
+    col_peers = peers_of_col(me_c, nc)
+    facet_peers = peers_of_facet(me_f, nf)
     height = ROWS * nc
     block = 2 * ROWS
 
@@ -144,17 +162,27 @@
 
     barrier = pltpu.get_barrier_semaphore()
 
-    def greet(axis, me, peers):
-        def one(k, carry):
-            pl.semaphore_signal(
-                barrier, 1, device_id={axis: lax.rem(me + k, peers)}, device_id_type=MESH
-            )
-            return carry
-
-        lax.fori_loop(1, peers, one, 0)
-
-    greet("col", me_c, nc)
-    greet("facet", me_f, nf)
+    for peer in col_peers:
+        pl.semaphore_signal(barrier, 1, device_id={"col": peer}, device_id_type=MESH)
+    for peer in facet_peers:
+        pl.semaphore_signal(barrier, 1, device_id={"facet": peer}, device_id_type=MESH)
+
+    local[0].wait()
+    pl.semaphore_wait(barrier, nc - 1 + nf - 1)
+
+    def remote(src, dst, send, recv, axis, peer):
+        return pltpu.make_async_remote_copy(
+            src_ref=src,
+            dst_ref=dst,
+            send_sem=send,
+            recv_sem=recv,
+            device_id={axis: peer},
+            device_id_type=MESH,
+        )
+
+    mine = slab.at[slab_rows(me_c)]
+    for peer in col_peers:
+        remote(mine, mine, slab_send, slab_recv, "col", peer).start()
 
     for copy in local[1:4]:
         copy.wait()
@@ -166,26 +194,6 @@
     cos, sin = unit_circle(iota((2 * XC, SLAB), 1) * (offset + (part & (XC - 1))))
     across_t[...] = (jnp.where(part < XC, cos, -sin) * (1.0 / math.sqrt(SLAB))).astype(BF16)
 
-    local[0].wait()
-    pl.semaphore_wait(barrier, nc - 1 + nf - 1)
-
-    def remote(src, dst, send, recv, axis, peer):
-        return pltpu.make_async_remote_copy(
-            src_ref=src,
-            dst_ref=dst,
-            send_sem=send,
-            recv_sem=recv,
-            device_id={axis: peer},
-            device_id_type=MESH,
-        )
-
-    def send_slab(k, carry):
-        mine = slab.at[slab_rows(me_c)]
-        remote(mine, mine, slab_send, slab_recv, "col", lax.rem(me_c + k, nc)).start()
-        return carry
-
-    lax.fori_loop(1, nc, send_slab, 0)
-
     lane_row = (8, 2 * height)
     place = iota(lane_row, 1)
     row_id = me_f * height + (place >> 1)
@@ -231,14 +239,10 @@
     spread = join_parts(dot(slab[...], across[...])).astype(BF16)
     c_out[...] = dot(phase[...], spread).astype(BF16)
 
-    def send_c(k, carry):
-        peer = lax.rem(me_f + k, nf)
+    for peer in facet_peers:
         remote(
             c_out.at[sub_rows(peer)], c_in.at[sub_rows(me_f)], c_send, c_recv.at[me_f], "facet", peer
         ).start()
-        return carry
-
-    lax.fori_loop(1, nf, send_c, 0)
     c_in[sub_rows(me_f), :] = c_out[sub_rows(me_f), :]
 
     lane_c = iota((XC, 2 * XC), 1)
@@ -298,14 +302,10 @@
         im = pltpu.roll(im, (XC + 128 - start) % 128, 1)
         r_out[pl.ds(f * XC, XC), :] = jnp.where(lane_c < XC, re, im).astype(BF16)
 
-    def send_r(k, carry):
-        peer = lax.rem(me_f + k, nf)
+    for peer in facet_peers:
         remote(
             r_out.at[sub_rows(peer)], r_in.at[sub_rows(me_f)], r_send, r_recv, "facet", peer
         ).start()
-        return carry
-
-    lax.fori_loop(1, nf, send_r, 0)
     r_in[sub_rows(me_f), :] = r_out[sub_rows(me_f), :]
 
     others = r_in.at[pl.ds(0, (nf - 1) * XC)]
@@ -314,14 +314,10 @@
     rows = join_parts(dot(phase_t[...], r_in[...])).astype(BF16)
     t_out[...] = dot(rows, across_t[...]).astype(BF16)
 
-    def send_t(k, carry):
-        peer = lax.rem(me_c + k, nc)
+    for peer in col_peers:
         remote(
             t_out.at[slab_rows(peer)], t_in.at[slab_rows(me_c)], t_send, t_recv, "col", peer
         ).start()
-        return carry
-
-    lax.fori_loop(1, nc, send_t, 0)
     t_in[slab_rows(me_c), :] = t_out[slab_rows(me_c), :]
 
     others = c_in.at[pl.ds(0, (nf - 1) * XC)]

time: 54.2 us -> 51.7 us (0.954)
  Pallas kernels: 51.4 us -> 48.9 us
    pallas_call x1, Pallas kernels: 51.4 us -> 48.9 us  [body(): pl.pallas_call(functools.partial(kernel, nf, nc), name='swiftly', out_sha...]
where the time goes in v1:
time: 51.7 us; the launch traced here: 51.5 us
  Pallas kernels  48.9 us (95%)
  local copies, waits for them, and re-layouts  1.3 us (3%)
  between operations  1.3 us (3%)
    pallas_call x1, Pallas kernels, body(): pl.pallas_call(functools.partial(kernel, nf, nc), name='swiftly', out_sha...  48.9 us
    unnamed x1, local copies, waits for them, and re-layouts  1.3 us

profile of v1, /device:TPU:1, one launch (start us, length us, event | category | flops | bytes accessed | tf_op | source)
XLA Modules:
  0.0 51.5 jit_solution(17895105596051970972)
XLA Ops:
  1.3 48.9 %swiftly.1 = f32[16,128]{1,0:T(8,128)} custom-call(bf16[16,128]{1,0:T(8,128)(2,1)} %bitcast.5, s32[1,16]{1,0:T(1,128)} %sub_hbm.1, s32[1,1]{1,0:T(1,128)} %bitcast.3.col_hbm, s32[1,1]{1,0:T(1,128)S(6)} %copy.12.idx_hbm, f32[4,2,256,256]{3,2,1,0:T(8,128)} %screens_hbm.1, bf16[512,512]{1,0:T(8,128)(2,1)} %constant.8.clone.row_in_hbm, ...), custom_call_target="tpu_custom_call" | custom-call | tf_op jit(solution)/shard_map/swiftly/pallas_call | solution.py:342
  50.2 1.3 %copy.13 = f32[1,8,2,128]{3,2,1,0:T(2,128)} copy(f32[1,8,2,128]{3,2,1,0:T(2,128)} %bitcast.4) | data formatting | bytes 16384

commit v2 on v1

--- a/solution.py
+++ b/solution.py
@@ -16,6 +16,7 @@
 STEP = 7
 ROWS = 8
 SPAN = 176
+BLOCKS = 3
 MESH = pl.DeviceIdType.MESH
 F32 = jnp.float32
 BF16 = jnp.bfloat16
@@ -28,10 +29,13 @@
     keep = (q < STEP * (facets - 1) + XC).astype(np.float64)
     re = np.cos(angle) / math.sqrt(XS) * keep
     im = np.sin(angle) / math.sqrt(XS) * keep
-    row_in = np.block([[re.T, im.T], [-im.T, re.T]])
+    across = np.block([[re.T, im.T], [-im.T, re.T]])
+    order = np.arange(BLOCKS * 2 * XC)
+    order = order // (2 * XC) * XC + order % XC + order // XC % 2 * XS
+    row_in = across[order]
     col_in = np.concatenate([re, im], axis=0) / math.sqrt(facets)
     col_out = np.concatenate([re.T[:SPAN], im.T[:SPAN]], axis=0)
-    row_out = np.block([[re, -im], [im, re]])
+    row_out = np.block([[re, -im], [im, re]])[:, order]
     return tuple(jnp.asarray(t, dtype=BF16) for t in (row_in, col_in, col_out, row_out))
 
 
@@ -78,7 +82,7 @@
 def peers_of_facet(me, count):
     nz = count // 2
     steps = [(dx, dz) for dx in range(2) for dz in range(nz) if dx or dz]
-    steps.sort(key=lambda k: -(min(k[1], nz - k[1]) + 2 * k[0]))
+    steps.sort(key=lambda k: (-k[0], -min(k[1], nz - k[1])))
     x, z = me // nz, lax.rem(me, nz)
     return [(x ^ dx) * nz + lax.rem(z + dz, nz) for dx, dz in steps]
 
@@ -88,8 +92,8 @@
     nc,
     x_hbm,
     sub_hbm,
-    col_hbm,
-    idx_hbm,
+    col_s,
+    idx_s,
     screens_hbm,
     row_in_hbm,
     col_in_hbm,
@@ -97,8 +101,6 @@
     row_out_hbm,
     out_ref,
     sub_s,
-    col_s,
-    idx_s,
     screens,
     row_in,
     col_in,
@@ -108,7 +110,8 @@
     phase,
     phase_t,
     across,
-    across_t,
+    offs,
+    back,
     c_out,
     c_in,
     z,
@@ -121,6 +124,8 @@
     local_sem,
     slab_send,
     slab_recv,
+    offs_send,
+    offs_recv,
     c_send,
     c_recv,
     r_send,
@@ -147,8 +152,6 @@
             [
                 (x_hbm, slab.at[slab_rows(me_c)]),
                 (sub_hbm, sub_s),
-                (col_hbm, col_s),
-                (idx_hbm, idx_s),
                 (screens_hbm, screens),
                 (row_in_hbm, row_in),
                 (col_in_hbm, col_in),
@@ -160,6 +163,10 @@
     for copy in local:
         copy.start()
 
+    offset = col_s[0]
+    shift = STEP * me_f
+    offs[me_c] = jnp.full((1, SLAB), offset, jnp.int32)
+
     barrier = pltpu.get_barrier_semaphore()
 
     for peer in col_peers:
@@ -184,16 +191,11 @@
     for peer in col_peers:
         remote(mine, mine, slab_send, slab_recv, "col", peer).start()
 
-    for copy in local[1:4]:
-        copy.wait()
-    offset = col_s[0, 0]
     lane = iota((SLAB, 2 * XC), 1)
-    cos, sin = unit_circle(iota((SLAB, 2 * XC), 0) * (offset + (lane & (XC - 1))))
+    cos, sin = unit_circle(iota((SLAB, 2 * XC), 0) * (offset + ((lane - shift) & (XC - 1))))
     across[...] = (jnp.where(lane < XC, cos, -sin) * (1.0 / math.sqrt(SLAB))).astype(BF16)
-    part = iota((2 * XC, SLAB), 0)
-    cos, sin = unit_circle(iota((2 * XC, SLAB), 1) * (offset + (part & (XC - 1))))
-    across_t[...] = (jnp.where(part < XC, cos, -sin) * (1.0 / math.sqrt(SLAB))).astype(BF16)
-
+
+    local[1].wait()
     lane_row = (8, 2 * height)
     place = iota(lane_row, 1)
     row_id = me_f * height + (place >> 1)
@@ -214,8 +216,10 @@
     lax.fori_loop(0, nf, fill_phase, 0)
 
     tall = (2 * height, 2 * XC)
-    row_t = me_f * height + (iota(tall, 0) >> 1)
-    turn_t = (iota(tall, 0) & 1) * (NPAD // 4)
+    place_t = iota(tall, 0)
+    second_t = place_t >= height
+    row_t = me_f * height + jnp.where(second_t, place_t - height, place_t)
+    turn_t = jnp.where(second_t, NPAD // 4, 0)
     lane_t = iota(tall, 1)
 
     def fill_phase_t(t, carry):
@@ -228,7 +232,7 @@
     lax.fori_loop(0, nf // 2, fill_phase_t, 0)
     z[...] = jnp.zeros_like(z)
     half[...] = jnp.zeros_like(half)
-    for copy in local[4:]:
+    for copy in local[2:]:
         copy.wait()
 
     others = slab.at[pl.ds(0, (nc - 1) * block)]
@@ -237,17 +241,30 @@
     arrival.wait_recv()
 
     spread = join_parts(dot(slab[...], across[...])).astype(BF16)
-    c_out[...] = dot(phase[...], spread).astype(BF16)
-
-    for peer in facet_peers:
-        remote(
-            c_out.at[sub_rows(peer)], c_in.at[sub_rows(me_f)], c_send, c_recv.at[me_f], "facet", peer
-        ).start()
+    half_rows = nf // 2 * XC
+    far_half = (me_f // (nf // 2)) ^ 1
+    for group in range(2):
+        rows = pl.ds(pl.multiple_of((far_half ^ group) * half_rows, half_rows), half_rows)
+        c_out[rows, :] = dot(phase[rows, :], spread).astype(BF16)
+        for peer in facet_peers[nf // 2 * group : nf // 2 * (group + 1)]:
+            remote(
+                c_out.at[sub_rows(peer)],
+                c_in.at[sub_rows(me_f)],
+                c_send,
+                c_recv.at[me_f],
+                "facet",
+                peer,
+            ).start()
     c_in[sub_rows(me_f), :] = c_out[sub_rows(me_f), :]
 
-    lane_c = iota((XC, 2 * XC), 1)
+    mine = offs.at[me_c]
+    for peer in col_peers:
+        remote(mine, mine, offs_send, offs_recv, "col", peer).start()
+
+    lane_v = iota((XC, 2 * XC), 1) & (XC - 1)
     for f in range(nf):
         start = STEP * f
+        first, inside = divmod(start, XC)
         rows = pl.ds(start, XC)
 
         @pl.when(f != me_f)
@@ -256,17 +273,14 @@
             remote(slot, slot, c_send, c_recv.at[f], "facet", me_f).wait_recv()
 
         got = c_in[pl.ds(f * XC, XC), :].astype(F32)
-        re = pltpu.roll(got, start, 1) if start else got
-        im = pltpu.roll(got, (start + XC) % (2 * XC), 1)
-        first = (lane_c >= start) & (lane_c < start + XC)
-        z[rows, 0:128] += jnp.where(first, re, 0.0)
-        z[rows, 256:384] += jnp.where(first, im, 0.0)
-        if start + XC > 128:
-            second = lane_c < start + XC - 128
-            z[rows, 128:256] += jnp.where(second, re, 0.0)
-            z[rows, 384:512] += jnp.where(second, im, 0.0)
-
-    half[0:SPAN, :] = dot(z[...].astype(BF16), row_in[...]).astype(BF16)
+        if inside:
+            z[first, rows, :] += jnp.where(lane_v >= inside, got, 0.0)
+            z[first + 1, rows, :] += jnp.where(lane_v >= inside, 0.0, got)
+        else:
+            z[first, rows, :] += got
+
+    placed = jnp.concatenate([z[b].astype(BF16) for b in range(BLOCKS)], axis=1)
+    half[0:SPAN, :] = dot(placed, row_in[...]).astype(BF16)
     grid = dot(col_in[...], half[...])
     sub_re = grid[0:XS, 0:XS] - grid[XS:, XS:]
     sub_im = grid[0:XS, XS:] + grid[XS:, 0:XS]
@@ -288,19 +302,18 @@
         ],
         axis=1,
     )
-    w[...] = dot(inner, row_out[...])
+    windows = dot(inner, row_out[...])
+    for b in range(BLOCKS):
+        w[b] = windows[:, b * 2 * XC : (b + 1) * 2 * XC]
 
     for f in range(nf):
         start = STEP * f
+        first, inside = divmod(start, XC)
         rows = pl.ds(start, XC)
-        re = w[rows, 0:128]
-        im = w[rows, 256:384]
-        if start + XC > 128:
-            re = jnp.where(lane_c >= start, re, w[rows, 128:256])
-            im = jnp.where(lane_c >= start, im, w[rows, 384:512])
-        re = pltpu.roll(re, 128 - start, 1) if start else re
-        im = pltpu.roll(im, (XC + 128 - start) % 128, 1)
-        r_out[pl.ds(f * XC, XC), :] = jnp.where(lane_c < XC, re, im).astype(BF16)
+        cut = w[first, rows, :]
+        if inside:
+            cut = jnp.where(lane_v >= inside, cut, w[first + 1, rows, :])
+        r_out[pl.ds(f * XC, XC), :] = cut.astype(BF16)
 
     for peer in facet_peers:
         remote(
@@ -308,28 +321,54 @@
         ).start()
     r_in[sub_rows(me_f), :] = r_out[sub_rows(me_f), :]
 
+    others = offs.at[pl.ds(0, nc - 1)]
+    arrival = remote(others, others, offs_send, offs_recv, "col", me_c)
+    arrival.wait_send()
+    arrival.wait_recv()
+    at_x = iota((XC, SLAB), 1)
+    at_v = (iota((XC, SLAB), 0) - shift) & (XC - 1)
+
+    def fill_across(j, carry):
+        cos_j, sin_j = unit_circle(at_x * (offs[j] + at_v))
+        cos_j = cos_j * (1.0 / math.sqrt(SLAB))
+        sin_j = sin_j * (1.0 / math.sqrt(SLAB))
+        back[j, 0:XC, 0:SLAB] = cos_j.astype(BF16)
+        back[j, 0:XC, SLAB:] = sin_j.astype(BF16)
+        back[j, XC:, 0:SLAB] = (-sin_j).astype(BF16)
+        back[j, XC:, SLAB:] = cos_j.astype(BF16)
+        return carry
+
+    lax.fori_loop(0, nc, fill_across, 0)
+
     others = r_in.at[pl.ds(0, (nf - 1) * XC)]
     remote(others, others, r_send, r_recv, "facet", me_f).wait_recv()
 
-    rows = join_parts(dot(phase_t[...], r_in[...])).astype(BF16)
-    t_out[...] = dot(rows, across_t[...]).astype(BF16)
-
+    terms = dot(phase_t[...], r_in[...])
+    turned = pltpu.roll(terms[height:], XC, 1)
+    rows = terms[0:height] + jnp.where(iota((height, 2 * XC), 1) < XC, -turned, turned)
+    t_out[...] = rows.reshape(nc, ROWS, 2 * XC).astype(BF16)
     for peer in col_peers:
-        remote(
-            t_out.at[slab_rows(peer)], t_in.at[slab_rows(me_c)], t_send, t_recv, "col", peer
-        ).start()
-    t_in[slab_rows(me_c), :] = t_out[slab_rows(me_c), :]
+        remote(t_out.at[peer], t_in.at[me_c], t_send, t_recv.at[me_c], "col", peer).start()
 
     others = c_in.at[pl.ds(0, (nf - 1) * XC)]
     remote(others, others, c_send, r_recv, "facet", me_f).wait_send()
     remote(others, others, r_send, r_recv, "facet", me_f).wait_send()
-    others = t_in.at[pl.ds(0, (nc - 1) * block)]
-    arrival = remote(others, others, t_send, t_recv, "col", me_c)
-    arrival.wait_send()
-    arrival.wait_recv()
-
-    total = jnp.sum(t_in[...].astype(F32).reshape(nc, block, SLAB), axis=0)
-    out_ref[...] = total * (1.0 / math.sqrt(nc * nf))
+
+    total = dot(t_out[me_c], back[me_c])
+    near_first = col_peers[::-1]
+    cut = 3 * nc // 4
+    for group in (near_first[:cut], near_first[cut:]):
+        for peer in group:
+            slot = t_in.at[peer]
+            remote(slot, slot, t_send, t_recv.at[peer], "col", me_c).wait_recv()
+        for peer in group:
+            total += dot(t_in[peer], back[peer])
+    total = total * (1.0 / math.sqrt(nc * nf))
+    out_ref[pl.ds(0, ROWS, stride=2), :] = total[:, 0:SLAB]
+    out_ref[pl.ds(1, ROWS, stride=2), :] = total[:, SLAB:]
+
+    others = t_in.at[pl.ds(0, nc - 1)]
+    remote(others, others, t_send, r_recv, "col", me_c).wait_send()
 
 
 def body(nf, nc, facets, sub_offsets, col_offsets, screen_index, screens):
@@ -337,35 +376,37 @@
     height = ROWS * nc
     tables = fourier_tables(nf)
     hbm = pl.BlockSpec(memory_space=pltpu.HBM)
+    smem = pl.BlockSpec(memory_space=pltpu.SMEM)
     vmem = pltpu.VMEM
     dma = pltpu.SemaphoreType.DMA
     out = pl.pallas_call(
         functools.partial(kernel, nf, nc),
         name="swiftly",
         out_shape=jax.ShapeDtypeStruct((block, SLAB), F32),
-        in_specs=[hbm] * 9,
+        in_specs=[hbm, hbm, smem, smem] + [hbm] * 5,
         out_specs=pl.BlockSpec(memory_space=pltpu.VMEM),
         scratch_shapes=[
             pltpu.SMEM((1, nf), jnp.int32),
-            pltpu.SMEM((1, 1), jnp.int32),
-            pltpu.SMEM((1, 1), jnp.int32),
             vmem(screens.shape, F32),
             *[vmem(t.shape, BF16) for t in tables],
             vmem((2 * height, SLAB), BF16),
             vmem((nf * XC, 2 * height), BF16),
             vmem((2 * height, nf * XC), BF16),
             vmem((SLAB, 2 * XC), BF16),
-            vmem((2 * XC, SLAB), BF16),
+            vmem((nc, 1, SLAB), jnp.int32),
+            vmem((nc, 2 * XC, 2 * SLAB), BF16),
             vmem((nf * XC, 2 * XC), BF16),
             vmem((nf * XC, 2 * XC), BF16),
-            vmem((SPAN, 2 * XS), F32),
+            vmem((BLOCKS, SPAN, 2 * XC), F32),
             vmem((XS, 2 * XS), BF16),
-            vmem((SPAN, 2 * XS), F32),
+            vmem((BLOCKS, SPAN, 2 * XC), F32),
             vmem((nf * XC, 2 * XC), BF16),
             vmem((nf * XC, 2 * XC), BF16),
-            vmem((2 * height, SLAB), BF16),
-            vmem((2 * height, SLAB), BF16),
-            dma((9,)),
+            vmem((nc, ROWS, 2 * XC), BF16),
+            vmem((nc, ROWS, 2 * XC), BF16),
+            dma((7,)),
+            dma,
+            dma,
             dma,
             dma,
             dma,
@@ -373,13 +414,13 @@
             dma,
             dma,
             dma,
-            dma,
+            dma((nc,)),
         ],
         compiler_params=pltpu.CompilerParams(collective_id=0, has_side_effects=True),
     )(
         facets.reshape(block, SLAB),
         sub_offsets,
-        col_offsets.reshape(1, 1),
+        col_offsets,
         screen_index,
         screens,
         *tables,

time: 51.7 us -> 50.5 us (0.977)
  Pallas kernels: 48.9 us -> 47.7 us
    pallas_call x1, Pallas kernels: 48.9 us -> 47.7 us  [body(): pl.pallas_call(functools.partial(kernel, nf, nc), name='swiftly', out_sha...]
where the time goes in v2:
time: 50.5 us; the launch traced here: 50.3 us
  Pallas kernels  47.7 us (94%)
  local copies, waits for them, and re-layouts  1.3 us (3%)
  between operations  1.3 us (3%)
    pallas_call x1, Pallas kernels, body(): pl.pallas_call(functools.partial(kernel, nf, nc), name='swiftly', out_sha...  47.7 us
    unnamed x1, local copies, waits for them, and re-layouts  1.3 us

profile of v2, /device:TPU:1, one launch (start us, length us, event | category | flops | bytes accessed | tf_op | source)
XLA Modules:
  0.0 50.3 jit_solution(14731537496551240331)
XLA Ops:
  1.3 47.7 %swiftly.1 = f32[16,128]{1,0:T(8,128)} custom-call(bf16[16,128]{1,0:T(8,128)(2,1)} %bitcast.3, s32[1,16]{1,0:T(1,128)} %sub_hbm.1, s32[1]{0:T(128)S(6)} %copy.11.col_s, s32[1,1]{1,0:T(1,128)S(6)} %copy.12.idx_s, f32[4,2,256,256]{3,2,1,0:T(8,128)} %screens_hbm.1, bf16[384,512]{1,0:T(8,128)(2,1)} %constant.8.clone.row_in_hbm, ...), custom_call_target="tpu_custom_call" | custom-call | tf_op jit(solution)/shard_map/swiftly/pallas_call | solution.py:382
  49.0 1.3 %copy.13 = f32[1,8,2,128]{3,2,1,0:T(2,128)} copy(f32[1,8,2,128]{3,2,1,0:T(2,128)} %bitcast.2) | data formatting | bytes 16384

commit v3 on v2

--- a/solution.py
+++ b/solution.py
@@ -84,7 +84,9 @@
     steps = [(dx, dz) for dx in range(2) for dz in range(nz) if dx or dz]
     steps.sort(key=lambda k: (-k[0], -min(k[1], nz - k[1])))
     x, z = me // nz, lax.rem(me, nz)
-    return [(x ^ dx) * nz + lax.rem(z + dz, nz) for dx, dz in steps]
+    by_x = [(x ^ dx) * nz + lax.rem(z + dz, nz) for dx, dz in steps]
+    steps.sort(key=lambda k: -(min(k[1], nz - k[1]) + 2 * k[0]))
+    return by_x, [(x ^ dx) * nz + lax.rem(z + dz, nz) for dx, dz in steps]
 
 
 def kernel(
@@ -136,7 +138,7 @@
     me_f = lax.axis_index("facet")
     me_c = lax.axis_index("col")
     col_peers = peers_of_col(me_c, nc)
-    facet_peers = peers_of_facet(me_f, nf)
+    facet_peers, facet_far = peers_of_facet(me_f, nf)
     height = ROWS * nc
     block = 2 * ROWS
 
@@ -260,6 +262,25 @@
     mine = offs.at[me_c]
     for peer in col_peers:
         remote(mine, mine, offs_send, offs_recv, "col", peer).start()
+
+    others = offs.at[pl.ds(0, nc - 1)]
+    arrival = remote(others, others, offs_send, offs_recv, "col", me_c)
+    arrival.wait_send()
+    arrival.wait_recv()
+    at_x = iota((XC, SLAB), 1)
+    at_v = (iota((XC, SLAB), 0) - shift) & (XC - 1)
+
+    def fill_across(j, carry):
+        cos_j, sin_j = unit_circle(at_x * (offs[j] + at_v))
+        cos_j = cos_j * (1.0 / math.sqrt(SLAB))
+        sin_j = sin_j * (1.0 / math.sqrt(SLAB))
+        back[j, 0:XC, 0:SLAB] = cos_j.astype(BF16)
+        back[j, 0:XC, SLAB:] = sin_j.astype(BF16)
+        back[j, XC:, 0:SLAB] = (-sin_j).astype(BF16)
+        back[j, XC:, SLAB:] = cos_j.astype(BF16)
+        return carry
+
+    lax.fori_loop(0, nc, fill_across, 0)
 
     lane_v = iota((XC, 2 * XC), 1) & (XC - 1)
     for f in range(nf):
@@ -315,30 +336,11 @@
             cut = jnp.where(lane_v >= inside, cut, w[first + 1, rows, :])
         r_out[pl.ds(f * XC, XC), :] = cut.astype(BF16)
 
-    for peer in facet_peers:
+    for peer in facet_far:
         remote(
             r_out.at[sub_rows(peer)], r_in.at[sub_rows(me_f)], r_send, r_recv, "facet", peer
         ).start()
     r_in[sub_rows(me_f), :] = r_out[sub_rows(me_f), :]
-
-    others = offs.at[pl.ds(0, nc - 1)]
-    arrival = remote(others, others, offs_send, offs_recv, "col", me_c)
-    arrival.wait_send()
-    arrival.wait_recv()
-    at_x = iota((XC, SLAB), 1)
-    at_v = (iota((XC, SLAB), 0) - shift) & (XC - 1)
-
-    def fill_across(j, carry):
-        cos_j, sin_j = unit_circle(at_x * (offs[j] + at_v))
-        cos_j = cos_j * (1.0 / math.sqrt(SLAB))
-        sin_j = sin_j * (1.0 / math.sqrt(SLAB))
-        back[j, 0:XC, 0:SLAB] = cos_j.astype(BF16)
-        back[j, 0:XC, SLAB:] = sin_j.astype(BF16)
-        back[j, XC:, 0:SLAB] = (-sin_j).astype(BF16)
-        back[j, XC:, SLAB:] = cos_j.astype(BF16)
-        return carry
-
-    lax.fori_loop(0, nc, fill_across, 0)
 
     others = r_in.at[pl.ds(0, (nf - 1) * XC)]
     remote(others, others, r_send, r_recv, "facet", me_f).wait_recv()
@@ -376,6 +378,7 @@
     height = ROWS * nc
     tables = fourier_tables(nf)
     hbm = pl.BlockSpec(memory_space=pltpu.HBM)
+    in_hbm = functools.partial(pltpu.with_memory_space_constraint, memory_space=pltpu.HBM)
     smem = pl.BlockSpec(memory_space=pltpu.SMEM)
     vmem = pltpu.VMEM
     dma = pltpu.SemaphoreType.DMA
@@ -416,14 +419,14 @@
             dma,
             dma((nc,)),
         ],
-        compiler_params=pltpu.CompilerParams(collective_id=0, has_side_effects=True),
+        compiler_params=pltpu.CompilerParams(collective_id=0, has_side_effects=True, vmem_limit_bytes=40 * 2**20),
     )(
-        facets.reshape(block, SLAB),
-        sub_offsets,
+        in_hbm(facets.reshape(block, SLAB)),
+        in_hbm(sub_offsets),
         col_offsets,
         screen_index,
-        screens,
-        *tables,
+        in_hbm(screens),
+        *map(in_hbm, tables),
     )
     return out.reshape(1, ROWS, 2, SLAB)
 

time: 50.5 us -> 48.7 us (0.964)
  Pallas kernels: 47.7 us -> 46.7 us
  local copies, waits for them, and re-layouts: 1.3 us -> 0.6 us
    pallas_call x1, Pallas kernels: 47.7 us -> 46.7 us  [body(): pl.pallas_call(functools.partial(kernel, nf, nc), name='swiftly', out_sha...]
    unnamed x1, local copies, waits for them, and re-layouts: 1.3 us -> 0.6 us
where the time goes in v3:
time: 48.7 us; the launch traced here: 48.6 us
  Pallas kernels  46.7 us (96%)
  between operations  1.3 us (3%)
  local copies, waits for them, and re-layouts  0.6 us (1%)
    pallas_call x1, Pallas kernels, body(): pl.pallas_call(functools.partial(kernel, nf, nc), name='swiftly', out_sha...  46.7 us

profile of v3, /device:TPU:1, one launch (start us, length us, event | category | flops | bytes accessed | tf_op | source)
XLA Modules:
  0.0 48.6 jit_solution(16167547008546526598)
XLA Ops:
  1.3 46.7 %swiftly.1 = f32[16,128]{1,0:T(8,128)S(1)} custom-call(bf16[16,128]{1,0:T(8,128)(2,1)} %bitcast.3, s32[1,16]{1,0:T(1,128)} %sub_hbm.1, s32[1]{0:T(128)S(6)} %copy.11.col_s, s32[1,1]{1,0:T(1,128)S(6)} %copy.12.idx_s, f32[4,2,256,256]{3,2,1,0:T(8,128)} %screens_hbm.1, bf16[384,512]{1,0:T(8,128)(2,1)} %constant.8.clone.row_in_hbm, ...), custom_call_target="tpu_custom_call" | custom-call | tf_op jit(solution)/shard_map/swiftly/pallas_call | solution.py:385
  48.0 0.6 %copy.13 = f32[1,8,2,128]{3,2,1,0:T(2,128)} copy(f32[1,8,2,128]{3,2,1,0:T(2,128)S(1)} %bitcast.2) | data formatting | bytes 16384

commit v4 on v3

--- a/solution.py
+++ b/solution.py
@@ -15,6 +15,7 @@
 NPAD = 8192
 STEP = 7
 ROWS = 8
+NEAR = 3
 SPAN = 176
 BLOCKS = 3
 MESH = pl.DeviceIdType.MESH
@@ -86,7 +87,10 @@
     x, z = me // nz, lax.rem(me, nz)
     by_x = [(x ^ dx) * nz + lax.rem(z + dz, nz) for dx, dz in steps]
     steps.sort(key=lambda k: -(min(k[1], nz - k[1]) + 2 * k[0]))
-    return by_x, [(x ^ dx) * nz + lax.rem(z + dz, nz) for dx, dz in steps]
+    far = [(x ^ dx) * nz + lax.rem(z + dz, nz) for dx, dz in steps]
+    near = [p for p, (dx, dz) in zip(far, steps) if min(dz, nz - dz) + 2 * dx <= NEAR]
+    below = lax.rem(z + nz - 1, nz)
+    return by_x, far, near, [(x ^ 1) * nz + z, (x ^ 1) * nz + below, x * nz + below]
 
 
 def kernel(
@@ -124,6 +128,7 @@
     t_out,
     t_in,
     local_sem,
+    ready,
     slab_send,
     slab_recv,
     offs_send,
@@ -138,7 +143,7 @@
     me_f = lax.axis_index("facet")
     me_c = lax.axis_index("col")
     col_peers = peers_of_col(me_c, nc)
-    facet_peers, facet_far = peers_of_facet(me_f, nf)
+    facet_peers, facet_far, facet_near, told = peers_of_facet(me_f, nf)
     height = ROWS * nc
     block = 2 * ROWS
 
@@ -173,11 +178,11 @@
 
     for peer in col_peers:
         pl.semaphore_signal(barrier, 1, device_id={"col": peer}, device_id_type=MESH)
-    for peer in facet_peers:
+    for peer in facet_near:
         pl.semaphore_signal(barrier, 1, device_id={"facet": peer}, device_id_type=MESH)
 
     local[0].wait()
-    pl.semaphore_wait(barrier, nc - 1 + nf - 1)
+    pl.semaphore_wait(barrier, nc - 1 + len(facet_near))
 
     def remote(src, dst, send, recv, axis, peer):
         return pltpu.make_async_remote_copy(
@@ -192,6 +197,8 @@
     mine = slab.at[slab_rows(me_c)]
     for peer in col_peers:
         remote(mine, mine, slab_send, slab_recv, "col", peer).start()
+    for peer in told:
+        pl.semaphore_signal(ready, 1, device_id={"facet": peer}, device_id_type=MESH)
 
     lane = iota((SLAB, 2 * XC), 1)
     cos, sin = unit_circle(iota((SLAB, 2 * XC), 0) * (offset + ((lane - shift) & (XC - 1))))
@@ -242,6 +249,7 @@
     arrival.wait_send()
     arrival.wait_recv()
 
+    pl.semaphore_wait(ready, 3)
     spread = join_parts(dot(slab[...], across[...])).astype(BF16)
     half_rows = nf // 2 * XC
     far_half = (me_f // (nf // 2)) ^ 1
@@ -408,6 +416,7 @@
             vmem((nc, ROWS, 2 * XC), BF16),
             vmem((nc, ROWS, 2 * XC), BF16),
             dma((7,)),
+            pltpu.SemaphoreType.REGULAR,
             dma,
             dma,
             dma,

time: 48.7 us -> 47.8 us (0.982)
  Pallas kernels: 46.7 us -> 45.7 us
    pallas_call x1, Pallas kernels: 46.7 us -> 45.7 us  [body(): pl.pallas_call(functools.partial(kernel, nf, nc), name='swiftly', out_sha...]
where the time goes in v4:
time: 47.8 us; the launch traced here: 47.6 us
  Pallas kernels  45.7 us (96%)
  between operations  1.3 us (3%)
  local copies, waits for them, and re-layouts  0.6 us (1%)
    pallas_call x1, Pallas kernels, body(): pl.pallas_call(functools.partial(kernel, nf, nc), name='swiftly', out_sha...  45.7 us

profile of v4, /device:TPU:1, one launch (start us, length us, event | category | flops | bytes accessed | tf_op | source)
XLA Modules:
  0.0 47.6 jit_solution(8426142399722156465)
XLA Ops:
  1.3 45.7 %swiftly.1 = f32[16,128]{1,0:T(8,128)S(1)} custom-call(bf16[16,128]{1,0:T(8,128)(2,1)} %bitcast.3, s32[1,16]{1,0:T(1,128)} %sub_hbm.1, s32[1]{0:T(128)S(6)} %copy.11.col_s, s32[1,1]{1,0:T(1,128)S(6)} %copy.12.idx_s, f32[4,2,256,256]{3,2,1,0:T(8,128)} %screens_hbm.1, bf16[384,512]{1,0:T(8,128)(2,1)} %constant.8.clone.row_in_hbm, ...), custom_call_target="tpu_custom_call" | custom-call | tf_op jit(solution)/shard_map/swiftly/pallas_call | solution.py:393
  47.0 0.6 %copy.13 = f32[1,8,2,128]{3,2,1,0:T(2,128)} copy(f32[1,8,2,128]{3,2,1,0:T(2,128)S(1)} %bitcast.2) | data formatting | bytes 16384

commit v5 on v4

--- a/solution.py
+++ b/solution.py
@@ -251,12 +251,15 @@
 
     pl.semaphore_wait(ready, 3)
     spread = join_parts(dot(slab[...], across[...])).astype(BF16)
-    half_rows = nf // 2 * XC
-    far_half = (me_f // (nf // 2)) ^ 1
-    for group in range(2):
-        rows = pl.ds(pl.multiple_of((far_half ^ group) * half_rows, half_rows), half_rows)
+    part = nf // 4
+    part_rows = part * XC
+    mine, inside = me_f // part, lax.rem(me_f, part)
+    for group in range(4):
+        first = (mine ^ (3 - group)) * part
+        rows = pl.ds(pl.multiple_of(first * XC, part_rows), part_rows)
         c_out[rows, :] = dot(phase[rows, :], spread).astype(BF16)
-        for peer in facet_peers[nf // 2 * group : nf // 2 * (group + 1)]:
+        for step in range(1 if group == 3 else 0, part):
+            peer = first + lax.rem(inside + step, part)
             remote(
                 c_out.at[sub_rows(peer)],
                 c_in.at[sub_rows(me_f)],
@@ -335,19 +338,27 @@
     for b in range(BLOCKS):
         w[b] = windows[:, b * 2 * XC : (b + 1) * 2 * XC]
 
-    for f in range(nf):
-        start = STEP * f
-        first, inside = divmod(start, XC)
-        rows = pl.ds(start, XC)
-        cut = w[first, rows, :]
-        if inside:
-            cut = jnp.where(lane_v >= inside, cut, w[first + 1, rows, :])
-        r_out[pl.ds(f * XC, XC), :] = cut.astype(BF16)
-
-    for peer in facet_far:
-        remote(
-            r_out.at[sub_rows(peer)], r_in.at[sub_rows(me_f)], r_send, r_recv, "facet", peer
-        ).start()
+    def cut_windows(low):
+        for f in range(low, low + nf // 2):
+            start = STEP * f
+            block_q, inside_q = divmod(start, XC)
+            rows_q = pl.ds(start, XC)
+            piece = w[block_q, rows_q, :]
+            if inside_q:
+                piece = jnp.where(lane_v >= inside_q, piece, w[block_q + 1, rows_q, :])
+            r_out[pl.ds(f * XC, XC), :] = piece.astype(BF16)
+
+    for group in range(2):
+        for half_x in range(2):
+
+            @pl.when((me_f // (nf // 2)) ^ (1 - group) == half_x)
+            def _():
+                cut_windows(half_x * (nf // 2))
+
+        for peer in facet_peers[nf // 2 * group : nf // 2 * (group + 1)]:
+            remote(
+                r_out.at[sub_rows(peer)], r_in.at[sub_rows(me_f)], r_send, r_recv, "facet", peer
+            ).start()
     r_in[sub_rows(me_f), :] = r_out[sub_rows(me_f), :]
 
     others = r_in.at[pl.ds(0, (nf - 1) * XC)]

time: 47.8 us -> 47.7 us (level)
  no operation moved by 1% of the time
where the time goes in v5:
time: 47.7 us; the launch traced here: 47.6 us
  Pallas kernels  45.7 us (96%)
  between operations  1.3 us (3%)
  local copies, waits for them, and re-layouts  0.6 us (1%)
    pallas_call x1, Pallas kernels, body(): pl.pallas_call(functools.partial(kernel, nf, nc), name='swiftly', out_sha...  45.7 us

profile of v5, /device:TPU:1, one launch (start us, length us, event | category | flops | bytes accessed | tf_op | source)
XLA Modules:
  0.0 47.6 jit_solution(13637389236583388108)
XLA Ops:
  1.3 45.7 %swiftly.1 = f32[16,128]{1,0:T(8,128)S(1)} custom-call(bf16[16,128]{1,0:T(8,128)(2,1)} %bitcast.3, s32[1,16]{1,0:T(1,128)} %sub_hbm.1, s32[1]{0:T(128)S(6)} %copy.11.col_s, s32[1,1]{1,0:T(1,128)S(6)} %copy.12.idx_s, f32[4,2,256,256]{3,2,1,0:T(8,128)} %screens_hbm.1, bf16[384,512]{1,0:T(8,128)(2,1)} %constant.8.clone.row_in_hbm, ...), custom_call_target="tpu_custom_call" | custom-call | tf_op jit(solution)/shard_map/swiftly/pallas_call | solution.py:404
  47.0 0.6 %copy.13 = f32[1,8,2,128]{3,2,1,0:T(2,128)} copy(f32[1,8,2,128]{3,2,1,0:T(2,128)S(1)} %bitcast.2) | data formatting | bytes 16384
